TPU v7x, 32 devices: a whole 2x2x4 slice. The times are simulated.
32 devices in a mesh: lon: 8 (over y, x, core), dp: 4 (over z).
Axes of the slice: x: 2, y: 2, z: 4, core: 2. Of those that a mesh axis runs over, the one named last changes fastest.
Arguments:
- inputs: bfloat16 [4, 32, 384, 256], P('dp', None, 'lon'), may hold values from -6 to 6
- pre_act: bfloat16 [4, 32, 384, 256], P('dp', None, 'lon'), may hold values from -6 to 6
- cotangent: bfloat16 [4, 32, 384, 256], P('dp', None, 'lon'), may hold values from -6 to 6
- first_weight: bfloat16 [2304, 256], replicated, may hold values from -0.125 to 0.125
- second_weight: bfloat16 [2304, 256], replicated, may hold values from -0.125 to 0.125
Outputs:
- input_gradient_array: bfloat16 [4, 32, 384, 256], P('dp', None, 'lon')
- first_weight_gradient: float32 [589824], P(('lon', 'dp'))
- second_weight_gradient: float32 [589824], P(('lon', 'dp'))
All inputs are finite; a program needn't handle non-finite values.
Results may differ from a plain program's by a relative error of at most 0.0049.
Values may be sent and summed in bfloat16 or wider, within the bound.
A program may use at most 64 MiB of HBM per device.

v0:
```python
import jax
import jax.numpy as jnp
from jax import lax
from jax.sharding import PartitionSpec as P

FIRST_SPREAD = 12
SECOND_SPREAD = 18


def with_halo(block, sides, width):
    for axis, dim in sides:
        count = lax.axis_size(axis)
        forward = [(i, i + 1) for i in range(count - 1)]
        forward.append((count - 1, 0))
        backward = [(target, source) for source, target in forward]
        low = lax.ppermute(
            lax.slice_in_dim(block, block.shape[dim] - width, None, axis=dim), axis, forward
        )
        high = lax.ppermute(lax.slice_in_dim(block, 0, width, axis=dim), axis, backward)
        block = jnp.concatenate([low, block, high], axis=dim)
    return block


def lat_move(values, offset):
    rows = values.shape[1]
    if offset == 0:
        return values
    blank = jnp.zeros_like(values[:, : abs(offset)])
    if offset > 0:
        return jnp.concatenate([values[:, offset:], blank], axis=1)
    return jnp.concatenate([blank, values[:, : rows + offset]], axis=1)


def tap_view(padded, border_width, dilation, tap, direction, start_offset, length):
    lat_off = direction * (tap // 3 - 1) * dilation
    lon_off = direction * (tap % 3 - 1) * dilation
    first_col = border_width + start_offset + lon_off
    return lat_move(padded[:, :, first_col : first_col + length], lat_off)


def weight_partials(padded, border_width, dilation, upstream):
    chans = upstream.shape[3]
    column_patches = upstream.shape[2]
    flat_up = upstream.reshape(-1, chans)
    blocks = []
    for tap in range(9):
        moved = tap_view(padded, border_width, dilation, tap, 1, 0, column_patches).reshape(
            -1, padded.shape[3]
        )
        blocks.append(jnp.dot(moved.T, flat_up, preferred_element_type=jnp.float32))
    return jnp.concatenate(blocks, axis=0)


def backprop_input(padded, border_width, dilation, weights, start_offset, length):
    chans = weights.shape[1]
    total = jnp.zeros((padded.shape[0] * padded.shape[1] * length, chans), jnp.float32)
    for tap in range(9):
        moved = tap_view(padded, border_width, dilation, tap, -1, start_offset, length).reshape(
            -1, chans
        )
        block = weights[tap * chans : (tap + 1) * chans]
        total = total + jnp.dot(moved, block.T, preferred_element_type=jnp.float32)
    return total.reshape(padded.shape[0], padded.shape[1], length, chans)


def local(inputs, pre_act, cotangent, first_weight, second_weight):
    column_patches = inputs.shape[2]
    norm_factor = float(
        inputs.shape[0]
        * inputs.shape[1]
        * column_patches
        * lax.axis_size("lon")
        * lax.axis_size("dp")
    ) ** (-0.5)
    input_padded = with_halo(inputs, (("lon", 2),), FIRST_SPREAD)
    stacked_patches = jnp.stack((pre_act, cotangent))
    border_width = SECOND_SPREAD
    border_strips = with_halo(stacked_patches, (("lon", 3),), SECOND_SPREAD)
    start_offset = 0
    pre_pad = border_strips[0]
    hidden_padded = jnp.maximum(pre_pad, jnp.zeros_like(pre_pad))
    second_output = (
        weight_partials(hidden_padded, border_width, SECOND_SPREAD, cotangent) * norm_factor
    )
    hidden_gradient = backprop_input(
        border_strips[1], border_width, SECOND_SPREAD, second_weight, start_offset, column_patches
    )
    pre_cols = pre_pad[
        :, :, border_width + start_offset : border_width + start_offset + column_patches
    ]
    partial_gradient = jnp.where(pre_cols > 0, hidden_gradient, jnp.float32(0.0)).astype(
        jnp.bfloat16
    )
    gradient_padded = with_halo(partial_gradient, (("lon", 2),), FIRST_SPREAD)
    interior_gradient = gradient_padded[:, :, FIRST_SPREAD : FIRST_SPREAD + column_patches]
    first_output = (
        weight_partials(input_padded, FIRST_SPREAD, FIRST_SPREAD, interior_gradient) * norm_factor
    )
    input_gradient_array = backprop_input(
        gradient_padded, FIRST_SPREAD, FIRST_SPREAD, first_weight, 0, column_patches
    ).astype(jnp.bfloat16)
    first_flat = first_output.reshape(-1)
    second_flat = second_output.reshape(-1)
    part_first, part_second = (
        lax.psum_scatter(first_flat, "lon", scatter_dimension=0, tiled=True),
        lax.psum_scatter(second_flat, "lon", scatter_dimension=0, tiled=True),
    )
    first_weight_gradient, second_weight_gradient = (
        lax.psum_scatter(part_first, "dp", scatter_dimension=0, tiled=True),
        lax.psum_scatter(part_second, "dp", scatter_dimension=0, tiled=True),
    )
    return (input_gradient_array, first_weight_gradient, second_weight_gradient)


def solution(mesh):
    in_specs = (
        P("dp", None, "lon", None),
        P("dp", None, "lon", None),
        P("dp", None, "lon", None),
        P(),
        P(),
    )
    out_specs = (P("dp", None, "lon", None), P(("lon", "dp")), P(("lon", "dp")))
    return jax.shard_map(local, mesh=mesh, in_specs=in_specs, out_specs=out_specs, check_vma=False)
```

profile of v0, /device:TPU:0, one launch (start us, length us, event | category | flops | bytes accessed | tf_op | source)
XLA Modules:
  0.0 203.3 jit_solution(4328432883689027759)
XLA Ops:
  7.2 2.0 fusion.125
  9.2 3.4 %collective-permute-start.5 = (bf16[1,32,12,256]{3,2,1,0:T(8,128)(2,1)}, bf16[1,32,12,256]{3,2,1,0:T(8,128)(2,1)}, u32[]{:S(2)}, u32[]{:S(2)}) collective-permute-start(bf16[1,32,12,256]{3,2,1,0:T(8,128)(2,1)} %get-tuple-element.35), channel_id=1, source_target_pairs={{4,0},{8,4},{12,8},{16,12},{20,16},{24,20},{28,24},{0,28},{5,1},{9... | collective-permute-start | bytes 589832 | tf_op jit(solution)/shard_map/ppermute | solution.py:19
  12.5 1.5 fusion.30
  14.4 2.7 %collective-permute-start.1 = (bf16[2,1,32,18,256]{4,2,3,1,0:T(8,128)(2,1)S(1)}, bf16[2,1,32,18,256]{4,2,3,1,0:T(8,128)(2,1)}, u32[]{:S(2)}, u32[]{:S(2)}) collective-permute-start(bf16[2,1,32,18,256]{4,2,3,1,0:T(8,128)(2,1)S(1)} %copy.9), channel_id=1, source_target_pairs={{4,0},{8,4},{12,8},{16,12},{20,16},{24,20},{28,24},{0,28},{5,1},{9... | collective-permute-start | bytes 1769480 | tf_op jit(solution)/shard_map/ppermute | solution.py:19
  17.1 0.6 dynamic-slice
  17.7 0.6 dynamic-slice.2
  19.7 1.0 constant_dynamic-update-slice_fusion
  20.7 0.4 fusion.123
  21.1 12.6 %collective-permute-done.4 = bf16[1,32,12,256]{3,2,1,0:T(8,128)(2,1)} collective-permute-done((bf16[1,32,12,256]{3,2,1,0:T(8,128)(2,1)}, bf16[1,32,12,256]{3,2,1,0:T(8,128)(2,1)}, u32[]{:S(2)}, u32[]{:S(2)}) %collective-permute-start.4) | collective-permute-done | bytes 196640 | tf_op jit(solution)/shard_map/ppermute | solution.py:16
  33.7 1.1 fusion.124
  35.2 1.4 copy.11
  36.6 1.6 pad_maximum_fusion
  38.4 0.6 fusion.121
  39.0 0.9 fusion.122
  40.4 1.1 copy-done.3
  41.9 0.4 convolution_add_fusion.15
  42.7 0.4 convolution_add_fusion.13
  43.1 0.4 convolution_add_fusion.12
  44.7 0.4 convolution_add_fusion.8
  45.1 0.5 select_convert_fusion
  46.9 1.4 fusion.21
  48.2 0.4 fusion.20
  48.7 0.4 fusion.19
  49.1 1.3 fusion.18
  50.5 0.4 fusion.17
  50.9 0.4 fusion.16
  51.5 2.7 %copy.12 = f32[288,2,8,128]{3,1,2,0:T(2,128)} copy(f32[288,2,8,128]{3,2,1,0:T(8,128)S(1)} %multiply_bitcast_fusion.1) | data formatting | bytes 4718592
  54.2 0.6 fusion.120
  56.0 0.4 fusion.12
  56.4 0.4 fusion.11
  56.9 0.4 fusion.10
  57.4 0.5 collective-permute-start.3
  59.2 2.7 %copy.13 = f32[288,2,8,128]{3,1,2,0:T(2,128)} copy(f32[288,2,8,128]{3,2,1,0:T(8,128)S(1)} %multiply_bitcast_fusion) | data formatting | bytes 4718592
  62.0 1.3 collective-permute-done.2
  63.3 2.1 %collective-permute-done.3 = bf16[1,32,12,256]{3,2,1,0:T(8,128)(2,1)S(1)} collective-permute-done((bf16[1,32,12,256]{3,2,1,0:T(8,128)(2,1)S(1)}, bf16[1,32,12,256]{3,2,1,0:T(8,128)(2,1)S(1)}, u32[]{:S(2)}, u32[]{:S(2)}) %collective-permute-start.3) | collective-permute-done | bytes 196640 | tf_op jit(solution)/shard_map/ppermute | solution.py:16
  65.4 0.4 fusion.126
  65.9 3.1 %fusion.32 = (bf16[1,32,48,256]{3,2,1,0:T(8,128)(2,1)S(1)}, bf16[1,32,48,256]{3,2,1,0:T(8,128)(2,1)S(1)}, bf16[1,32,48,256]{3,2,1,0:T(8,128)(2,1)S(1)}, bf16[1,32,48,256]{3,2,1,0:T(8,128)(2,1)S(1)}) fusion(bf16[1,32,48,256]{3,2,1,0:T(8,128)(2,1)S(1)} %select_convert_fusion, bf16[1,32,12,256]{3,2,1,0:T(8,128)(2,1)S(1)} %collective-permute-done.3, ...), kind=kLoop, calls=%fused_computation.87 | loop fusion | flops 8257536 | bytes 4325376 | tf_op jit(solution)/shard_map/concatenate | solution.py:20
  69.3 1.2 copy-done.4
  70.9 0.4 convolution_add_fusion.7
  72.5 0.4 convolution_add_fusion.3
  73.3 76.7 %all-reduce.33.cloned.1.call-done = (f32[589824]{0:T(1024)}, f32[589824]{0:T(1024)}) async-done(((f32[589824]{0:T(1024)}, f32[589824]{0:T(1024)}), (f32[589824]{0:T(1024)}, f32[589824]{0:T(1024)})) %all-reduce.33.cloned.1.call-update) | async-done | bytes 4718608
  150.0 1.7 dynamic-slice.1
  151.7 1.7 dynamic-slice.5
  153.5 1.3 convolution_add_fusion.1
  154.8 2.2 %fusion = bf16[1536,256]{1,0:T(8,128)(2,1)} fusion(f32[1536,256]{1,0:T(8,128)S(1)} %convolution_add_fusion.1, bf16[1536,256]{1,0:T(8,128)(2,1)S(1)} %bitcast.237, bf16[2304,256]{1,0:T(8,128)(2,1)} %param.8), kind=kOutput, calls=%fused_computation.17 | convolution fusion | flops 202113024 | bytes 3276800 | tf_op jit(solution)/shard_map/dot_general | solution.py:62
  157.0 36.5 %all-reduce.35.cloned.1.call-done = (f32[73728]{0:T(1024)}, f32[73728]{0:T(1024)}) async-done(((f32[73728]{0:T(1024)}, f32[73728]{0:T(1024)}), (f32[73728]{0:T(1024)}, f32[73728]{0:T(1024)})) %all-reduce.35.cloned.1.call-update) | async-done | bytes 589840
  193.5 1.5 dynamic-slice.7
  195.0 1.5 dynamic-slice.3
  (60 shorter events, 9.7 us)
Async XLA Ops:
  7.2 5.4 %copy-start.1 = (bf16[1,32,48,256]{3,2,1,0:T(8,128)(2,1)S(1)}, bf16[1,32,48,256]{3,2,1,0:T(8,128)(2,1)}, u32[]{:S(2)}) copy-start(bf16[1,32,48,256]{3,2,1,0:T(8,128)(2,1)} %param.6) | copy-start | bytes 2359300
  7.2 142.9 %all-reduce.33.cloned.1.call-start = ((), (), s32[]{:S(2)}) async-start(), calls=%async_computation | async-start | bytes 9437184
  9.2 10.5 %collective-permute-start.5 = (bf16[1,32,12,256]{3,2,1,0:T(8,128)(2,1)}, bf16[1,32,12,256]{3,2,1,0:T(8,128)(2,1)}, u32[]{:S(2)}, u32[]{:S(2)}) collective-permute-start(bf16[1,32,12,256]{3,2,1,0:T(8,128)(2,1)} %get-tuple-element.35), channel_id=1, source_target_pairs={{4,0},{8,4},{12,8},{16,12},{20,16},{24,20},{28,24},{0,28},{5,1},{9... | collective-permute-start | bytes 589832 | tf_op jit(solution)/shard_map/ppermute | solution.py:19
  14.1 3.1 %copy-start.6 = (u32[32]{0:T(128)S(1)}, u32[32]{0:T(128)}, u32[]{:S(2)}) copy-start(u32[32]{0:T(128)} %constant.62) | copy-start | bytes 388
  14.1 3.6 %copy-start.5 = (u32[32]{0:T(128)S(1)}, u32[32]{0:T(128)}, u32[]{:S(2)}) copy-start(u32[32]{0:T(128)} %constant.66) | copy-start | bytes 388
  14.1 5.5 %copy-start = (bf16[1,32,48,256]{3,2,1,0:T(8,128)(2,1)S(1)}, bf16[1,32,48,256]{3,2,1,0:T(8,128)(2,1)}, u32[]{:S(2)}) copy-start(bf16[1,32,48,256]{3,2,1,0:T(8,128)(2,1)} %param.5) | copy-start | bytes 2359300
  14.2 20.6 %collective-permute-start = (bf16[2,1,32,18,256]{4,2,3,1,0:T(8,128)(2,1)S(1)}, bf16[2,1,32,18,256]{4,2,3,1,0:T(8,128)(2,1)S(1)}, u32[]{:S(2)}, u32[]{:S(2)}) collective-permute-start(bf16[2,1,32,18,256]{4,2,3,1,0:T(8,128)(2,1)S(1)} %copy.8), channel_id=1, source_target_pairs={{0,4},{4,8},{8,12},{12,16},{16,20},{20,24},{24,28},{28,0},{1,5},{5... | collective-permute-start | bytes 1769480 | tf_op jit(solution)/shard_map/ppermute | solution.py:16
  14.4 20.8 %collective-permute-start.1 = (bf16[2,1,32,18,256]{4,2,3,1,0:T(8,128)(2,1)S(1)}, bf16[2,1,32,18,256]{4,2,3,1,0:T(8,128)(2,1)}, u32[]{:S(2)}, u32[]{:S(2)}) collective-permute-start(bf16[2,1,32,18,256]{4,2,3,1,0:T(8,128)(2,1)S(1)} %copy.9), channel_id=1, source_target_pairs={{4,0},{8,4},{12,8},{16,12},{20,16},{24,20},{28,24},{0,28},{5,1},{9... | collective-permute-start | bytes 1769480 | tf_op jit(solution)/shard_map/ppermute | solution.py:19
  17.1 16.6 %collective-permute-start.4 = (bf16[1,32,12,256]{3,2,1,0:T(8,128)(2,1)}, bf16[1,32,12,256]{3,2,1,0:T(8,128)(2,1)}, u32[]{:S(2)}, u32[]{:S(2)}) collective-permute-start(bf16[1,32,12,256]{3,2,1,0:T(8,128)(2,1)} %get-tuple-element.36), channel_id=1, source_target_pairs={{0,4},{4,8},{8,12},{12,16},{16,20},{20,24},{24,28},{28,0},{1,5},{5... | collective-permute-start | bytes 589832 | tf_op jit(solution)/shard_map/ppermute | solution.py:16
  34.8 1.8 copy-start.2
  40.2 1.3 copy-start.3
  57.3 6.1 %collective-permute-start.2 = (bf16[1,32,12,256]{3,2,1,0:T(8,128)(2,1)S(1)}, bf16[1,32,12,256]{3,2,1,0:T(8,128)(2,1)S(1)}, u32[]{:S(2)}, u32[]{:S(2)}) collective-permute-start(bf16[1,32,12,256]{3,2,1,0:T(8,128)(2,1)S(1)} %get-tuple-element.44), channel_id=1, source_target_pairs={{4,0},{8,4},{12,8},{16,12},{20,16},{24,20},{28,24},{0,28},{5,1},{9... | collective-permute-start | bytes 589832 | tf_op jit(solution)/shard_map/ppermute | solution.py:19
  57.4 8.1 %collective-permute-start.3 = (bf16[1,32,12,256]{3,2,1,0:T(8,128)(2,1)S(1)}, bf16[1,32,12,256]{3,2,1,0:T(8,128)(2,1)S(1)}, u32[]{:S(2)}, u32[]{:S(2)}) collective-permute-start(bf16[1,32,12,256]{3,2,1,0:T(8,128)(2,1)S(1)} %get-tuple-element.43), channel_id=1, source_target_pairs={{0,4},{4,8},{8,12},{12,16},{16,20},{20,24},{24,28},{28,0},{1,5},{5... | collective-permute-start | bytes 589832 | tf_op jit(solution)/shard_map/ppermute | solution.py:16
  62.0 131.5 %all-reduce.35.cloned.1.call-start = ((), (), s32[]{:S(2)}) async-start(), calls=%async_computation.1 | async-start | bytes 1179648
  69.2 1.3 copy-start.4
Sparse Core Ops, SparseCore 0:
  62.1 87.9 all-reduce.32
  153.6 39.8 all-reduce.34
where the time goes:
time: 204 us; the launch traced here: 203 us
  waiting for transfers between devices  129 us (63%)
  local copies, waits for them, and re-layouts  23.7 us (12%)
  matrix products  19 us (9%)
  between operations  15.9 us (8%)
  other arithmetic  8.78 us (4%)
  starting transfers between devices  6.74 us (3%)
    unnamed x4, waiting for transfers between devices  113 us
    unnamed x23, local copies, waits for them, and re-layouts  15.4 us
    ppermute x3, waiting for transfers between devices, with_halo(): lax.ppermute(lax.slice_in_dim(block, block.shape[dim] - width, None, axis...  14.7 us
    dot_general x18, matrix products, backprop_input(): total = total + jnp.dot(moved, block.T, preferred_element_type=jnp.float32)  9.91 us
    dot_general x18, matrix products, weight_partials(): blocks.append(jnp.dot(moved.T, flat_up, preferred_element_type=jnp.float32))  9.1 us
    ppermute x3, starting transfers between devices, with_halo(): lax.ppermute(lax.slice_in_dim(block, 0, width, axis=dim), axis, backward)  6.1 us
    concatenate x2, other arithmetic, with_halo(): block = jnp.concatenate([low, block, high], axis=dim)  4.71 us
  transfers between devices with their start and end apart: 8, of which 5 were waited for; matrix products, arithmetic and copies ran while one was open for 10% of the time, Pallas kernels for 0%

commit v1 on v0

v1 whole, which is shorter than its diff:
```python
import functools

import jax
import jax.numpy as jnp
from jax import lax
from jax.experimental import pallas as pl
from jax.experimental.pallas import tpu as pltpu
from jax.sharding import PartitionSpec as P

FIRST_SPREAD = 12
SECOND_SPREAD = 18
MESH = pl.DeviceIdType.MESH
F32 = jnp.float32
BF16 = jnp.bfloat16
LANE_SLOT = (0, 2, 1)


def row_span(rows, dilation, r):
    if r == 0:
        return 0, rows - dilation, dilation
    if r == 1:
        return 0, rows, 0
    return dilation, rows, 0


def dot_nt(a, b):
    return lax.dot_general(a, b, (((1,), (1,)), ((), ())), preferred_element_type=F32)


def dot_tn(a, b):
    return lax.dot_general(a, b, (((0,), (0,)), ((), ())), preferred_element_type=F32)


def flat(v):
    return v.reshape(-1, v.shape[-1])


def kernel(nl, nd, scatter, norm, *refs):
    inp, pre, cot, w1, w2 = refs[:5]
    ig_out, g1_out, g2_out = refs[5:8]
    (cot_v, pre_v, inp_v, lg_v, ig_v, w1_v, w2_v, side2, side1, acc) = refs[8:18]
    (in_sem, w1_sem, w2_sem, out_sem) = refs[18:22]
    (s2_lo, s2_hi, r2_lo, r2_hi, s1_lo, s1_hi, r1_lo, r1_hi, hs_sem, hr_sem) = refs[22:32]
    if scatter:
        (dw1, dw2, ps1, ps2, pr1, pr2, as1, as2, ar1, ar2) = refs[32:42]
        (p_ssem, p_rsem, a_ssem, a_rsem) = refs[42:46]
    else:
        dw1, dw2 = g1_out, g2_out

    rows, cols, ch = cot_v.shape
    me_l, me_d = lax.axis_index("lon"), lax.axis_index("dp")
    left, right = lax.rem(me_l + nl - 1, nl), lax.rem(me_l + 1, nl)
    half = nl // 2
    slots = half * nd
    core = lax.rem(me_l, 2)
    my_slot = (me_l // 2) * nd + me_d

    def slot_device(slot):
        return (2 * (slot // nd) + core, lax.rem(slot, nd))

    load_cot = pltpu.make_async_copy(cot.at[0], cot_v, in_sem.at[0])
    load_pre = pltpu.make_async_copy(pre.at[0], pre_v, in_sem.at[1])
    load_inp = pltpu.make_async_copy(inp.at[0], inp_v, in_sem.at[2])

    def weight_loads(w, w_v, sem):
        return [
            pltpu.make_async_copy(
                w.at[pl.ds(k * ch, ch)],
                w_v.at[k // 3, :, pl.ds(LANE_SLOT.index(k % 3) * ch, ch)],
                sem.at[k],
            )
            for k in range(9)
        ]

    load_w2 = weight_loads(w2, w2_v, w2_sem)
    load_w1 = weight_loads(w1, w1_v, w1_sem)
    load_cot.start()
    for c in load_w2:
        c.start()
    load_pre.start()
    load_inp.start()
    for c in load_w1:
        c.start()

    barrier = pltpu.get_barrier_semaphore()
    for other in (left, right):
        pl.semaphore_signal(barrier, inc=1, device_id=(other, me_d), device_id_type=MESH)
    greeted = 2
    if scatter:

        def greet(t, _):
            pl.semaphore_signal(
                barrier,
                inc=1,
                device_id=slot_device(lax.rem(my_slot + t, slots)),
                device_id_type=MESH,
            )
            return 0

        lax.fori_loop(1, slots, greet, 0)
        greeted += slots - 1

    def halo_copies(lo, hi, from_right, from_left, base):
        return (
            pltpu.make_async_remote_copy(
                src_ref=lo, dst_ref=from_right, send_sem=hs_sem.at[base],
                recv_sem=hr_sem.at[base], device_id=(left, me_d), device_id_type=MESH,
            ),
            pltpu.make_async_remote_copy(
                src_ref=hi, dst_ref=from_left, send_sem=hs_sem.at[base + 1],
                recv_sem=hr_sem.at[base + 1], device_id=(right, me_d), device_id_type=MESH,
            ),
        )

    def pack(src, lo, hi, d):
        for p in range(rows):
            lo[p * d : (p + 1) * d, :] = src[p, 0:d, :]
            hi[p * d : (p + 1) * d, :] = src[p, cols - d : cols, :]

    def side_inner(src, side, d):
        side[:, 0 : cols - d, 0:ch] = src[:, d:cols, :]
        side[:, d:cols, ch : 2 * ch] = src[:, 0 : cols - d, :]

    def side_edges(side, from_right, from_left, d):
        side[:, cols - d : cols, 0:ch] = from_right[...].reshape(rows, d, ch)
        side[:, 0:d, ch : 2 * ch] = from_left[...].reshape(rows, d, ch)

    def input_terms(src, lanes, w_v, wl, d, fresh):
        for r in (1, 0, 2):
            lo, hi, first = row_span(rows, d, r)
            term = dot_nt(
                flat(src[first : first + hi - lo, :, 0:lanes]), w_v[r, :, wl : wl + lanes]
            )
            if fresh and r == 1:
                acc[...] = term
            else:
                acc[lo * cols : hi * cols, :] += term

    def weight_terms(x, src, lanes, dw, taps, d):
        for r in range(3):
            lo, hi, first = row_span(rows, d, r)
            term = dot_tn(flat(x[lo:hi]), flat(src[first : first + hi - lo, :, 0:lanes]))
            for at, c in enumerate(taps):
                k = 3 * r + c
                value = term[:, at * ch : (at + 1) * ch]
                dw[k * ch : (k + 1) * ch, :] = value if scatter else value * norm

    if scatter:
        depth = dw1.shape[0] // (nl * nd)

        def chunk_rows(slot, parity):
            l, d = 2 * (slot // nd) + parity, lax.rem(slot, nd)
            return pl.ds(pl.multiple_of((l * nd + d) * depth, 8), depth)

        def pair_copy(ps, pr, at):
            partner = me_l + 1 - 2 * core
            return pltpu.make_async_remote_copy(
                src_ref=ps, dst_ref=pr, send_sem=p_ssem.at[at], recv_sem=p_rsem.at[at],
                device_id=(partner, me_d), device_id_type=MESH,
            )

        def pair_pack(dw, ps):
            def one(s, _):
                v = dw[chunk_rows(s, 1 - core), :].astype(BF16)
                ps[s, 0:depth, :] = v[:, : ch // 2]
                ps[s, depth : 2 * depth, :] = v[:, ch // 2 :]
                return 0

            lax.fori_loop(0, slots, one, 0)

        def chip_sum(dw, pr, s):
            v = dw[chunk_rows(s, core), :]
            return (
                v[:, : ch // 2] + pr[s, 0:depth, :].astype(F32),
                v[:, ch // 2 :] + pr[s, depth : 2 * depth, :].astype(F32),
            )

        def spread_copy(a_s, a_r, at, t):
            slot = lax.rem(my_slot + t, slots)
            return pltpu.make_async_remote_copy(
                src_ref=a_s.at[slot], dst_ref=a_r.at[t], send_sem=a_ssem.at[at, t],
                recv_sem=a_rsem.at[at, t], device_id=slot_device(slot), device_id_type=MESH,
            )

        def spread(dw, pr, a_s, a_r, at):
            def fill(s, _):
                lo, hi = chip_sum(dw, pr, s)
                a_s[s, 0:depth, :] = lo.astype(BF16)
                a_s[s, depth : 2 * depth, :] = hi.astype(BF16)
                return 0

            lax.fori_loop(0, slots, fill, 0)

            def send(t, _):
                spread_copy(a_s, a_r, at, t).start()
                return 0

            lax.fori_loop(1, slots, send, 0)

        def gather_sum(dw, pr, a_s, a_r, at, out):
            def add(t, total):
                spread_copy(a_s, a_r, at, t).wait()
                return (
                    total[0] + a_r[t, 0:depth, :].astype(F32),
                    total[1] + a_r[t, depth : 2 * depth, :].astype(F32),
                )

            lo, hi = lax.fori_loop(1, slots, add, chip_sum(dw, pr, my_slot))
            out[pl.ds(0, depth, stride=2), :] = lo * norm
            out[pl.ds(1, depth, stride=2), :] = hi * norm

    load_cot.wait()
    pack(cot_v, s2_lo, s2_hi, SECOND_SPREAD)
    pl.semaphore_wait(barrier, greeted)
    halo2 = halo_copies(s2_lo, s2_hi, r2_lo, r2_hi, 0)
    for c in halo2:
        c.start()
    side_inner(cot_v, side2, SECOND_SPREAD)
    for c in load_w2:
        c.wait()
    input_terms(cot_v, ch, w2_v, 2 * ch, SECOND_SPREAD, True)
    load_pre.wait()
    zero = jnp.zeros((), BF16)
    pre_v[...] = jnp.maximum(pre_v[...], zero)
    weight_terms(pre_v, cot_v, ch, dw2, (1,), SECOND_SPREAD)
    for c in halo2:
        c.wait()
    side_edges(side2, r2_lo, r2_hi, SECOND_SPREAD)
    input_terms(side2, 2 * ch, w2_v, 0, SECOND_SPREAD, False)
    grad = jnp.where(flat(pre_v[...]) > 0, acc[...], F32(0.0)).astype(BF16)
    lg_v[...] = grad.reshape(rows, cols, ch)
    pack(lg_v, s1_lo, s1_hi, FIRST_SPREAD)
    halo1 = halo_copies(s1_lo, s1_hi, r1_lo, r1_hi, 2)
    for c in halo1:
        c.start()
    weight_terms(pre_v, side2, 2 * ch, dw2, (0, 2), SECOND_SPREAD)
    if scatter:
        pair_pack(dw2, ps2)
        pair2 = pair_copy(ps2, pr2, 0)
        pair2.start()

    load_inp.wait()
    side_inner(lg_v, side1, FIRST_SPREAD)
    weight_terms(inp_v, lg_v, ch, dw1, (1,), FIRST_SPREAD)
    if scatter:
        pair2.wait()
        spread(dw2, pr2, as2, ar2, 0)
    for c in halo1:
        c.wait()
    side_edges(side1, r1_lo, r1_hi, FIRST_SPREAD)
    weight_terms(inp_v, side1, 2 * ch, dw1, (0, 2), FIRST_SPREAD)
    if scatter:
        pair_pack(dw1, ps1)
        pair1 = pair_copy(ps1, pr1, 1)
        pair1.start()
    for c in load_w1:
        c.wait()
    input_terms(lg_v, ch, w1_v, 2 * ch, FIRST_SPREAD, True)
    if scatter:
        pair1.wait()
        spread(dw1, pr1, as1, ar1, 1)
    input_terms(side1, 2 * ch, w1_v, 0, FIRST_SPREAD, False)
    ig_v[...] = acc[...].astype(BF16).reshape(rows, cols, ch)
    store = pltpu.make_async_copy(ig_v, ig_out.at[0], out_sem)
    store.start()
    if scatter:
        gather_sum(dw2, pr2, as2, ar2, 0, g2_out)
        gather_sum(dw1, pr1, as1, ar1, 1, g1_out)
    store.wait()


def local(nl, nd, inputs, pre_act, cotangent, first_weight, second_weight):
    _, rows, cols, ch = inputs.shape
    taps_rows = first_weight.shape[0]
    norm = float(rows * cols * nl * inputs.shape[0] * nd) ** -0.5
    devices = nl * nd
    depth = taps_rows // devices
    scatter = nl % 2 == 0 and taps_rows % devices == 0 and depth % 8 == 0
    slots = devices // 2
    vm = pltpu.VMEM
    dma = pltpu.SemaphoreType.DMA
    field = vm((rows, cols, ch), BF16)
    edge2 = vm((rows * SECOND_SPREAD, ch), BF16)
    edge1 = vm((rows * FIRST_SPREAD, ch), BF16)
    weights = vm((3, ch, 3 * ch), BF16)
    side = vm((rows, cols, 2 * ch), BF16)
    scratch = [field] * 5 + [weights] * 2 + [side] * 2 + [vm((rows * cols, ch), F32)]
    scratch += [dma((3,)), dma((9,)), dma((9,)), dma]
    scratch += [edge2] * 4 + [edge1] * 4 + [dma((4,)), dma((4,))]
    if scatter:
        pieces = vm((slots, 2 * depth, ch // 2), BF16)
        scratch += [vm((taps_rows, ch), F32)] * 2 + [pieces] * 8
        scratch += [dma((2,)), dma((2,)), dma((2, slots)), dma((2, slots))]
        grad_shape = (2 * depth, ch // 2)
    else:
        grad_shape = (taps_rows, ch)
    any_spec = pl.BlockSpec(memory_space=pl.ANY)
    vmem_spec = pl.BlockSpec(memory_space=pltpu.VMEM)
    ig, g1, g2 = pl.pallas_call(
        functools.partial(kernel, nl, nd, scatter, norm),
        out_shape=(
            jax.ShapeDtypeStruct(inputs.shape, BF16),
            jax.ShapeDtypeStruct(grad_shape, F32),
            jax.ShapeDtypeStruct(grad_shape, F32),
        ),
        in_specs=[any_spec] * 5,
        out_specs=(any_spec, vmem_spec, vmem_spec),
        scratch_shapes=scratch,
        compiler_params=pltpu.CompilerParams(
            collective_id=0, has_side_effects=True, vmem_limit_bytes=48 * 1024 * 1024
        ),
        name="conv_backward",
    )(inputs, pre_act, cotangent, first_weight, second_weight)
    g1, g2 = g1.reshape(-1), g2.reshape(-1)
    if not scatter:
        g1, g2 = (lax.psum_scatter(g, "lon", scatter_dimension=0, tiled=True) for g in (g1, g2))
        g1, g2 = (lax.psum_scatter(g, "dp", scatter_dimension=0, tiled=True) for g in (g1, g2))
    return ig, g1, g2


def solution(mesh):
    in_specs = (
        P("dp", None, "lon", None),
        P("dp", None, "lon", None),
        P("dp", None, "lon", None),
        P(),
        P(),
    )
    out_specs = (P("dp", None, "lon", None), P(("lon", "dp")), P(("lon", "dp")))
    step = functools.partial(local, mesh.shape["lon"], mesh.shape["dp"])
    return jax.shard_map(step, mesh=mesh, in_specs=in_specs, out_specs=out_specs, check_vma=False)
```

time: 204 us -> 56.7 us (0.28)
  waiting for transfers between devices: 129 us -> 0 us
  Pallas kernels: 0 us -> 47.6 us
  matrix products: 19 us -> 0 us
  local copies, waits for them, and re-layouts: 23.7 us -> 8.09 us
  between operations: 15.9 us -> 0.65 us
  other arithmetic: 8.78 us -> 0 us
  starting transfers between devices: 6.74 us -> 0 us
    unnamed x4 -> x0, waiting for transfers between devices: 113 us -> none
    pallas_call x0 -> x1, Pallas kernels: none -> 47.6 us  [local(): pl.pallas_call(functools.partial(kernel, nl, nd, scatter, norm), out_shap...]
    dot_general x36 -> x0, matrix products: 19 us -> none  [the longest x18 9.91 us: backprop_input(): total = total + jnp.dot(moved, block.T, preferred_element_type=jnp.float32)]
    ppermute x6 -> x0, waiting for transfers between devices: 16 us -> none  [the longest x3 14.7 us: with_halo(): lax.ppermute(lax.slice_in_dim(block, block.shape[dim] - width, None, axis...]
    unnamed x23 -> x13, local copies, waits for them, and re-layouts: 15.4 us -> 8.09 us
    ppermute x6 -> x0, starting transfers between devices: 6.66 us -> none  [the longest x3 6.1 us: with_halo(): lax.ppermute(lax.slice_in_dim(block, 0, width, axis=dim), axis, backward)]
    slice x8 -> x0, local copies, waits for them, and re-layouts: 4.85 us -> none  [the longest x2 2.08 us: with_halo(): lax.slice_in_dim(block, 0, width, axis=dim)]
    concatenate x2 -> x0, other arithmetic: 4.71 us -> none  [with_halo(): block = jnp.concatenate([low, block, high], axis=dim)]
  transfers between devices with their start and end apart: 8 -> 0, of which waited for: 5 -> 0; matrix products, arithmetic and copies ran while one was open for 10% -> 0% of each run, Pallas kernels for 0% -> 0%
where the time goes in v1:
time: 56.7 us; the launch traced here: 56.4 us
  Pallas kernels  47.6 us (84%)
  local copies, waits for them, and re-layouts  8.09 us (14%)
  between operations  0.65 us (1%)
    pallas_call x1, Pallas kernels, local(): pl.pallas_call(functools.partial(kernel, nl, nd, scatter, norm), out_shap...  47.6 us
    unnamed x13, local copies, waits for them, and re-layouts  8.09 us

profile of v1, /device:TPU:0, one launch (start us, length us, event | category | flops | bytes accessed | tf_op | source)
XLA Modules:
  0.0 56.4 jit_solution(1663939682989421023)
XLA Ops:
  0.6 0.0 copy-start
  0.6 1.3 %copy-done = bf16[2304,256]{1,0:T(8,128)(2,1)S(1)} copy-done((bf16[2304,256]{1,0:T(8,128)(2,1)S(1)}, bf16[2304,256]{1,0:T(8,128)(2,1)}, u32[]{:S(2)}) %copy-start) | copy-done | bytes 1179672
  1.9 0.0 copy-start.1
  1.9 1.3 %copy-done.1 = bf16[2304,256]{1,0:T(8,128)(2,1)S(1)} copy-done((bf16[2304,256]{1,0:T(8,128)(2,1)S(1)}, bf16[2304,256]{1,0:T(8,128)(2,1)}, u32[]{:S(2)}) %copy-start.1) | copy-done | bytes 1179672
  3.2 0.0 copy-start.2
  3.2 1.1 %copy-done.2 = bf16[1,32,48,256]{3,2,1,0:T(8,128)(2,1)S(1)} copy-done((bf16[1,32,48,256]{3,2,1,0:T(8,128)(2,1)S(1)}, bf16[1,32,48,256]{3,2,1,0:T(8,128)(2,1)}, u32[]{:S(2)}) %copy-start.2) | copy-done | bytes 786456
  4.3 0.0 copy-start.3
  4.3 1.1 %copy-done.3 = bf16[1,32,48,256]{3,2,1,0:T(8,128)(2,1)S(1)} copy-done((bf16[1,32,48,256]{3,2,1,0:T(8,128)(2,1)S(1)}, bf16[1,32,48,256]{3,2,1,0:T(8,128)(2,1)}, u32[]{:S(2)}) %copy-start.3) | copy-done | bytes 786456
  5.4 0.0 copy-start.4
  5.4 1.1 %copy-done.4 = bf16[1,32,48,256]{3,2,1,0:T(8,128)(2,1)S(1)} copy-done((bf16[1,32,48,256]{3,2,1,0:T(8,128)(2,1)S(1)}, bf16[1,32,48,256]{3,2,1,0:T(8,128)(2,1)}, u32[]{:S(2)}) %copy-start.4) | copy-done | bytes 786456
  6.6 47.6 %conv_backward.1 = (bf16[1,32,48,256]{3,2,1,0:T(8,128)(2,1)S(1)}, f32[144,128]{1,0:T(8,128)S(1)}, f32[144,128]{1,0:T(8,128)S(1)}) custom-call(bf16[1,32,48,256]{3,2,1,0:T(8,128)(2,1)S(1)} %copy-done.2, bf16[1,32,48,256]{3,2,1,0:T(8,128)(2,1)S(1)} %copy-done.3, bf16[1,32,48,256]{3,2,1,0:T(8,128)(2,1)S(1)} %copy-done.4, bf16[2304,256]{1,0:T(8,128)(2,1)S(1)} %copy-done, ...), custom_call_target="tpu_custom_call" | custom-call | tf_op jit(solution)/shard_map/conv_backward/pallas_call | solution.py:299
  54.2 0.9 %copy.11 = bf16[1,32,48,256]{3,2,1,0:T(8,128)(2,1)} copy(bf16[1,32,48,256]{3,2,1,0:T(8,128)(2,1)S(1)} %get-tuple-element.12) | data formatting | bytes 1572864
  55.1 0.6 %copy.12 = f32[18432]{0:T(1024)} copy(f32[18432]{0:T(1024)S(1)} %bitcast.3) | data formatting | bytes 147456
  55.7 0.6 %copy.13 = f32[18432]{0:T(1024)} copy(f32[18432]{0:T(1024)S(1)} %bitcast.2) | data formatting | bytes 147456
Async XLA Ops:
  0.6 1.3 %copy-start = (bf16[2304,256]{1,0:T(8,128)(2,1)S(1)}, bf16[2304,256]{1,0:T(8,128)(2,1)}, u32[]{:S(2)}) copy-start(bf16[2304,256]{1,0:T(8,128)(2,1)} %refs_3_.1) | copy-start | bytes 3538948
  1.9 1.3 %copy-start.1 = (bf16[2304,256]{1,0:T(8,128)(2,1)S(1)}, bf16[2304,256]{1,0:T(8,128)(2,1)}, u32[]{:S(2)}) copy-start(bf16[2304,256]{1,0:T(8,128)(2,1)} %refs_4_.1) | copy-start | bytes 3538948
  3.2 1.1 %copy-start.2 = (bf16[1,32,48,256]{3,2,1,0:T(8,128)(2,1)S(1)}, bf16[1,32,48,256]{3,2,1,0:T(8,128)(2,1)}, u32[]{:S(2)}) copy-start(bf16[1,32,48,256]{3,2,1,0:T(8,128)(2,1)} %refs_0_.1) | copy-start | bytes 2359300
  4.3 1.1 %copy-start.3 = (bf16[1,32,48,256]{3,2,1,0:T(8,128)(2,1)S(1)}, bf16[1,32,48,256]{3,2,1,0:T(8,128)(2,1)}, u32[]{:S(2)}) copy-start(bf16[1,32,48,256]{3,2,1,0:T(8,128)(2,1)} %refs_1_.1) | copy-start | bytes 2359300
  5.4 1.1 %copy-start.4 = (bf16[1,32,48,256]{3,2,1,0:T(8,128)(2,1)S(1)}, bf16[1,32,48,256]{3,2,1,0:T(8,128)(2,1)}, u32[]{:S(2)}) copy-start(bf16[1,32,48,256]{3,2,1,0:T(8,128)(2,1)} %refs_2_.1) | copy-start | bytes 2359300

commit v2 on v1

--- a/solution.py
+++ b/solution.py
@@ -43,7 +43,7 @@
     (s2_lo, s2_hi, r2_lo, r2_hi, s1_lo, s1_hi, r1_lo, r1_hi, hs_sem, hr_sem) = refs[22:32]
     if scatter:
         (dw1, dw2, ps1, ps2, pr1, pr2, as1, as2, ar1, ar2) = refs[32:42]
-        (p_ssem, p_rsem, a_ssem, a_rsem) = refs[42:46]
+        (zs1, zs2, zr1, zr2, p_ssem, p_rsem, a_ssem, a_rsem, z_ssem, z_rsem) = refs[42:52]
     else:
         dw1, dw2 = g1_out, g2_out
 
@@ -53,10 +53,14 @@
     half = nl // 2
     slots = half * nd
     core = lax.rem(me_l, 2)
-    my_slot = (me_l // 2) * nd + me_d
-
-    def slot_device(slot):
-        return (2 * (slot // nd) + core, lax.rem(slot, nd))
+
+    my_chip = me_l // 2
+
+    def plane_device(t):
+        return (2 * lax.rem(my_chip + t, half) + core, me_d)
+
+    def depth_device(u):
+        return (me_l, lax.rem(me_d + u, nd))
 
     load_cot = pltpu.make_async_copy(cot.at[0], cot_v, in_sem.at[0])
     load_pre = pltpu.make_async_copy(pre.at[0], pre_v, in_sem.at[1])
@@ -87,18 +91,11 @@
         pl.semaphore_signal(barrier, inc=1, device_id=(other, me_d), device_id_type=MESH)
     greeted = 2
     if scatter:
-
-        def greet(t, _):
-            pl.semaphore_signal(
-                barrier,
-                inc=1,
-                device_id=slot_device(lax.rem(my_slot + t, slots)),
-                device_id_type=MESH,
-            )
-            return 0
-
-        lax.fori_loop(1, slots, greet, 0)
-        greeted += slots - 1
+        for t in range(1, half):
+            pl.semaphore_signal(barrier, inc=1, device_id=plane_device(t), device_id_type=MESH)
+        for u in range(1, nd):
+            pl.semaphore_signal(barrier, inc=1, device_id=depth_device(u), device_id_type=MESH)
+        greeted += half - 1 + nd - 1
 
     def halo_copies(lo, hi, from_right, from_left, base):
         return (
@@ -147,26 +144,28 @@
 
     if scatter:
         depth = dw1.shape[0] // (nl * nd)
+        plane_order = (*range(1, half), 0)
 
         def chunk_rows(slot, parity):
             l, d = 2 * (slot // nd) + parity, lax.rem(slot, nd)
             return pl.ds(pl.multiple_of((l * nd + d) * depth, 8), depth)
 
-        def pair_copy(ps, pr, at):
-            partner = me_l + 1 - 2 * core
+        def pair_copy(ps, pr, at, t):
+            part = pl.ds(lax.rem(my_chip + t, half) * nd, nd)
             return pltpu.make_async_remote_copy(
-                src_ref=ps, dst_ref=pr, send_sem=p_ssem.at[at], recv_sem=p_rsem.at[at],
-                device_id=(partner, me_d), device_id_type=MESH,
-            )
-
-        def pair_pack(dw, ps):
-            def one(s, _):
-                v = dw[chunk_rows(s, 1 - core), :].astype(BF16)
-                ps[s, 0:depth, :] = v[:, : ch // 2]
-                ps[s, depth : 2 * depth, :] = v[:, ch // 2 :]
-                return 0
-
-            lax.fori_loop(0, slots, one, 0)
+                src_ref=ps.at[part], dst_ref=pr.at[part],
+                send_sem=p_ssem.at[at, t], recv_sem=p_rsem.at[at, t],
+                device_id=(me_l + 1 - 2 * core, me_d), device_id_type=MESH,
+            )
+
+        def pair_send(dw, ps, pr, at):
+            for t in plane_order:
+                for d in range(nd):
+                    s = lax.rem(my_chip + t, half) * nd + d
+                    v = dw[chunk_rows(s, 1 - core), :].astype(BF16)
+                    ps[s, 0:depth, :] = v[:, : ch // 2]
+                    ps[s, depth : 2 * depth, :] = v[:, ch // 2 :]
+                pair_copy(ps, pr, at, t).start()
 
         def chip_sum(dw, pr, s):
             v = dw[chunk_rows(s, core), :]
@@ -175,37 +174,57 @@
                 v[:, ch // 2 :] + pr[s, depth : 2 * depth, :].astype(F32),
             )
 
-        def spread_copy(a_s, a_r, at, t):
-            slot = lax.rem(my_slot + t, slots)
+        def plane_copy(a_s, a_r, at, t):
+            chip = lax.rem(my_chip + t, half)
             return pltpu.make_async_remote_copy(
-                src_ref=a_s.at[slot], dst_ref=a_r.at[t], send_sem=a_ssem.at[at, t],
-                recv_sem=a_rsem.at[at, t], device_id=slot_device(slot), device_id_type=MESH,
-            )
-
-        def spread(dw, pr, a_s, a_r, at):
-            def fill(s, _):
-                lo, hi = chip_sum(dw, pr, s)
-                a_s[s, 0:depth, :] = lo.astype(BF16)
-                a_s[s, depth : 2 * depth, :] = hi.astype(BF16)
-                return 0
-
-            lax.fori_loop(0, slots, fill, 0)
-
-            def send(t, _):
-                spread_copy(a_s, a_r, at, t).start()
-                return 0
-
-            lax.fori_loop(1, slots, send, 0)
-
-        def gather_sum(dw, pr, a_s, a_r, at, out):
-            def add(t, total):
-                spread_copy(a_s, a_r, at, t).wait()
-                return (
-                    total[0] + a_r[t, 0:depth, :].astype(F32),
-                    total[1] + a_r[t, depth : 2 * depth, :].astype(F32),
-                )
-
-            lo, hi = lax.fori_loop(1, slots, add, chip_sum(dw, pr, my_slot))
+                src_ref=a_s.at[pl.ds(chip * nd, nd)], dst_ref=a_r.at[pl.ds(t * nd, nd)],
+                send_sem=a_ssem.at[at, t], recv_sem=a_rsem.at[at, t],
+                device_id=plane_device(t), device_id_type=MESH,
+            )
+
+        def depth_copy(z_s, z_r, at, u):
+            return pltpu.make_async_remote_copy(
+                src_ref=z_s.at[lax.rem(me_d + u, nd)], dst_ref=z_r.at[u],
+                send_sem=z_ssem.at[at, u], recv_sem=z_rsem.at[at, u],
+                device_id=depth_device(u), device_id_type=MESH,
+            )
+
+        def spread(dw, ps, pr, a_s, a_r, at):
+            for t in plane_order:
+                pair_copy(ps, pr, at, t).wait()
+                if t == 0:
+                    continue
+                for d in range(nd):
+                    s = lax.rem(my_chip + t, half) * nd + d
+                    lo, hi = chip_sum(dw, pr, s)
+                    a_s[s, 0:depth, :] = lo.astype(BF16)
+                    a_s[s, depth : 2 * depth, :] = hi.astype(BF16)
+                plane_copy(a_s, a_r, at, t).start()
+
+        def plane_sum(dw, pr, a_r, d):
+            lo, hi = chip_sum(dw, pr, my_chip * nd + d)
+            for t in range(1, half):
+                lo += a_r[t * nd + d, 0:depth, :].astype(F32)
+                hi += a_r[t * nd + d, depth : 2 * depth, :].astype(F32)
+            return lo, hi
+
+        def across(dw, pr, a_s, a_r, z_s, z_r, at):
+            for t in range(1, half):
+                plane_copy(a_s, a_r, at, t).wait()
+
+            for u in range(1, nd):
+                d = lax.rem(me_d + u, nd)
+                lo, hi = plane_sum(dw, pr, a_r, d)
+                z_s[d, 0:depth, :] = lo.astype(BF16)
+                z_s[d, depth : 2 * depth, :] = hi.astype(BF16)
+                depth_copy(z_s, z_r, at, u).start()
+
+        def gather_sum(dw, pr, a_r, z_s, z_r, at, out):
+            lo, hi = plane_sum(dw, pr, a_r, me_d)
+            for u in range(1, nd):
+                depth_copy(z_s, z_r, at, u).wait()
+                lo += z_r[u, 0:depth, :].astype(F32)
+                hi += z_r[u, depth : 2 * depth, :].astype(F32)
             out[pl.ds(0, depth, stride=2), :] = lo * norm
             out[pl.ds(1, depth, stride=2), :] = hi * norm
 
@@ -235,37 +254,33 @@
         c.start()
     weight_terms(pre_v, side2, 2 * ch, dw2, (0, 2), SECOND_SPREAD)
     if scatter:
-        pair_pack(dw2, ps2)
-        pair2 = pair_copy(ps2, pr2, 0)
-        pair2.start()
+        pair_send(dw2, ps2, pr2, 0)
 
     load_inp.wait()
     side_inner(lg_v, side1, FIRST_SPREAD)
     weight_terms(inp_v, lg_v, ch, dw1, (1,), FIRST_SPREAD)
     if scatter:
-        pair2.wait()
-        spread(dw2, pr2, as2, ar2, 0)
+        spread(dw2, ps2, pr2, as2, ar2, 0)
     for c in halo1:
         c.wait()
     side_edges(side1, r1_lo, r1_hi, FIRST_SPREAD)
     weight_terms(inp_v, side1, 2 * ch, dw1, (0, 2), FIRST_SPREAD)
     if scatter:
-        pair_pack(dw1, ps1)
-        pair1 = pair_copy(ps1, pr1, 1)
-        pair1.start()
+        pair_send(dw1, ps1, pr1, 1)
     for c in load_w1:
         c.wait()
     input_terms(lg_v, ch, w1_v, 2 * ch, FIRST_SPREAD, True)
     if scatter:
-        pair1.wait()
-        spread(dw1, pr1, as1, ar1, 1)
+        spread(dw1, ps1, pr1, as1, ar1, 1)
+        across(dw2, pr2, as2, ar2, zs2, zr2, 0)
     input_terms(side1, 2 * ch, w1_v, 0, FIRST_SPREAD, False)
     ig_v[...] = acc[...].astype(BF16).reshape(rows, cols, ch)
     store = pltpu.make_async_copy(ig_v, ig_out.at[0], out_sem)
     store.start()
     if scatter:
-        gather_sum(dw2, pr2, as2, ar2, 0, g2_out)
-        gather_sum(dw1, pr1, as1, ar1, 1, g1_out)
+        across(dw1, pr1, as1, ar1, zs1, zr1, 1)
+        gather_sum(dw2, pr2, ar2, zs2, zr2, 0, g2_out)
+        gather_sum(dw1, pr1, ar1, zs1, zr1, 1, g1_out)
     store.wait()
 
 
@@ -290,7 +305,8 @@
     if scatter:
         pieces = vm((slots, 2 * depth, ch // 2), BF16)
         scratch += [vm((taps_rows, ch), F32)] * 2 + [pieces] * 8
-        scratch += [dma((2,)), dma((2,)), dma((2, slots)), dma((2, slots))]
+        scratch += [vm((nd, 2 * depth, ch // 2), BF16)] * 4
+        scratch += [dma((2, nl // 2))] * 4 + [dma((2, nd))] * 2
         grad_shape = (2 * depth, ch // 2)
     else:
         grad_shape = (taps_rows, ch)
@@ -307,7 +323,7 @@
         out_specs=(any_spec, vmem_spec, vmem_spec),
         scratch_shapes=scratch,
         compiler_params=pltpu.CompilerParams(
-            collective_id=0, has_side_effects=True, vmem_limit_bytes=48 * 1024 * 1024
+            collective_id=0, has_side_effects=True, vmem_limit_bytes=62 * 1024 * 1024
         ),
         name="conv_backward",
     )(inputs, pre_act, cotangent, first_weight, second_weight)

time: 56.7 us -> 43.7 us (0.77)
  Pallas kernels: 47.6 us -> 39.5 us
  local copies, waits for them, and re-layouts: 8.09 us -> 3.38 us
    pallas_call x1, Pallas kernels: 47.6 us -> 39.5 us  [local(): pl.pallas_call(functools.partial(kernel, nl, nd, scatter, norm), out_shap...]
    unnamed x13 -> x7, local copies, waits for them, and re-layouts: 8.09 us -> 3.38 us
where the time goes in v2:
time: 43.7 us; the launch traced here: 43.6 us
  Pallas kernels  39.5 us (90%)
  local copies, waits for them, and re-layouts  3.38 us (8%)
  between operations  0.66 us (2%)
    pallas_call x1, Pallas kernels, local(): pl.pallas_call(functools.partial(kernel, nl, nd, scatter, norm), out_shap...  39.5 us
    unnamed x7, local copies, waits for them, and re-layouts  3.38 us

profile of v2, /device:TPU:0, one launch (start us, length us, event | category | flops | bytes accessed | tf_op | source)
XLA Modules:
  0.0 43.6 jit_solution(1988447406553250573)
XLA Ops:
  0.6 39.5 %conv_backward.1 = (bf16[1,32,48,256]{3,2,1,0:T(8,128)(2,1)}, f32[144,128]{1,0:T(8,128)}, f32[144,128]{1,0:T(8,128)}) custom-call(bf16[1,32,48,256]{3,2,1,0:T(8,128)(2,1)} %refs_0_.1, bf16[1,32,48,256]{3,2,1,0:T(8,128)(2,1)} %refs_1_.1, bf16[1,32,48,256]{3,2,1,0:T(8,128)(2,1)} %refs_2_.1, bf16[2304,256]{1,0:T(8,128)(2,1)} %refs_3_.1, bf16[2304,256]{1,0:T(8,128)(2,1)} %refs_4_.1), custom_call_target="tpu_custom_call" | custom-call | tf_op jit(solution)/shard_map/conv_backward/pallas_call | solution.py:315
  40.2 0.0 copy-start.1
  40.2 0.0 copy-start
  40.2 2.1 %copy.11 = bf16[1,32,48,256]{3,2,1,0:T(8,128)(2,1)} copy(bf16[1,32,48,256]{3,2,1,0:T(8,128)(2,1)} %get-tuple-element.12) | data formatting | bytes 1572864
  42.3 0.0 copy-done.1
  42.3 0.6 %copy.12 = f32[18432]{0:T(1024)} copy(f32[18432]{0:T(1024)S(1)} %bitcast.3) | data formatting | bytes 147456
  42.9 0.0 copy-done
  42.9 0.6 %copy.13 = f32[18432]{0:T(1024)} copy(f32[18432]{0:T(1024)S(1)} %bitcast.2) | data formatting | bytes 147456
Async XLA Ops:
  40.2 2.1 %copy-start.1 = (f32[144,128]{1,0:T(8,128)S(1)}, f32[144,128]{1,0:T(8,128)}, u32[]{:S(2)}) copy-start(f32[144,128]{1,0:T(8,128)} %get-tuple-element.7) | copy-start | bytes 221188
  40.2 2.8 %copy-start = (f32[144,128]{1,0:T(8,128)S(1)}, f32[144,128]{1,0:T(8,128)}, u32[]{:S(2)}) copy-start(f32[144,128]{1,0:T(8,128)} %get-tuple-element.8) | copy-start | bytes 221188

commit v3 on v2

--- a/solution.py
+++ b/solution.py
@@ -144,7 +144,7 @@
 
     if scatter:
         depth = dw1.shape[0] // (nl * nd)
-        plane_order = (*range(1, half), 0)
+        plane_order = (*range(1, half, 2), *range(2, half, 2), 0)
 
         def chunk_rows(slot, parity):
             l, d = 2 * (slot // nd) + parity, lax.rem(slot, nd)
@@ -248,10 +248,13 @@
     input_terms(side2, 2 * ch, w2_v, 0, SECOND_SPREAD, False)
     grad = jnp.where(flat(pre_v[...]) > 0, acc[...], F32(0.0)).astype(BF16)
     lg_v[...] = grad.reshape(rows, cols, ch)
-    pack(lg_v, s1_lo, s1_hi, FIRST_SPREAD)
     halo1 = halo_copies(s1_lo, s1_hi, r1_lo, r1_hi, 2)
-    for c in halo1:
-        c.start()
+    for p in range(rows):
+        s1_lo[p * FIRST_SPREAD : (p + 1) * FIRST_SPREAD, :] = lg_v[p, 0:FIRST_SPREAD, :]
+    halo1[0].start()
+    for p in range(rows):
+        s1_hi[p * FIRST_SPREAD : (p + 1) * FIRST_SPREAD, :] = lg_v[p, cols - FIRST_SPREAD : cols, :]
+    halo1[1].start()
     weight_terms(pre_v, side2, 2 * ch, dw2, (0, 2), SECOND_SPREAD)
     if scatter:
         pair_send(dw2, ps2, pr2, 0)

time: 43.7 us -> 43.8 us (level)
  no operation moved by 1% of the time
where the time goes in v3:
time: 43.8 us; the launch traced here: 43.6 us
  Pallas kernels  39.6 us (90%)
  local copies, waits for them, and re-layouts  3.38 us (8%)
  between operations  0.66 us (2%)
    pallas_call x1, Pallas kernels, local(): pl.pallas_call(functools.partial(kernel, nl, nd, scatter, norm), out_shap...  39.6 us
    unnamed x7, local copies, waits for them, and re-layouts  3.38 us

profile of v3, /device:TPU:0, one launch (start us, length us, event | category | flops | bytes accessed | tf_op | source)
XLA Modules:
  0.0 43.6 jit_solution(1552744590914256610)
XLA Ops:
  0.6 39.6 %conv_backward.1 = (bf16[1,32,48,256]{3,2,1,0:T(8,128)(2,1)}, f32[144,128]{1,0:T(8,128)}, f32[144,128]{1,0:T(8,128)}) custom-call(bf16[1,32,48,256]{3,2,1,0:T(8,128)(2,1)} %refs_0_.1, bf16[1,32,48,256]{3,2,1,0:T(8,128)(2,1)} %refs_1_.1, bf16[1,32,48,256]{3,2,1,0:T(8,128)(2,1)} %refs_2_.1, bf16[2304,256]{1,0:T(8,128)(2,1)} %refs_3_.1, bf16[2304,256]{1,0:T(8,128)(2,1)} %refs_4_.1), custom_call_target="tpu_custom_call" | custom-call | tf_op jit(solution)/shard_map/conv_backward/pallas_call | solution.py:318
  40.2 0.0 copy-start.1
  40.3 0.0 copy-start
  40.3 2.1 %copy.11 = bf16[1,32,48,256]{3,2,1,0:T(8,128)(2,1)} copy(bf16[1,32,48,256]{3,2,1,0:T(8,128)(2,1)} %get-tuple-element.12) | data formatting | bytes 1572864
  42.4 0.0 copy-done.1
  42.4 0.6 %copy.12 = f32[18432]{0:T(1024)} copy(f32[18432]{0:T(1024)S(1)} %bitcast.3) | data formatting | bytes 147456
  43.0 0.0 copy-done
  43.0 0.6 %copy.13 = f32[18432]{0:T(1024)} copy(f32[18432]{0:T(1024)S(1)} %bitcast.2) | data formatting | bytes 147456
Async XLA Ops:
  40.2 2.1 %copy-start.1 = (f32[144,128]{1,0:T(8,128)S(1)}, f32[144,128]{1,0:T(8,128)}, u32[]{:S(2)}) copy-start(f32[144,128]{1,0:T(8,128)} %get-tuple-element.7) | copy-start | bytes 221188
  40.3 2.8 %copy-start = (f32[144,128]{1,0:T(8,128)S(1)}, f32[144,128]{1,0:T(8,128)}, u32[]{:S(2)}) copy-start(f32[144,128]{1,0:T(8,128)} %get-tuple-element.8) | copy-start | bytes 221188
